TPU v7x, 32 devices: a whole 2x2x4 slice. The times are simulated.
32 devices in a mesh: owner: 4 (over x, core), rows: 8 (over z, y).
Axes of the slice: x: 2, y: 2, z: 4, core: 2. Of those that a mesh axis runs over, the one named last changes fastest.
Arguments:
- w_down: float32 [16, 6400, 4096], P('owner', None, 'rows'), may hold values from -0.109375 to 0.109375
- avg_down: bfloat16 [16, 6400, 4096], P('owner', None, 'rows'), may hold values from -0.0390625 to 0.0390625
- router_weight: float32 [4096, 16], P('rows', 'owner'), may hold values from -0.09375 to 0.09375
- router_gain: float32 [4096], P('rows'), may hold values from 0.25 to 1.75
Outputs:
- serve_down: bfloat16 [16, 6400, 4096], P('owner', 'rows')
- scale_down: float32 [16, 6400], P('owner', 'rows')
- serve_router: bfloat16 [4096, 16], replicated
All inputs are finite; a program needn't handle non-finite values. Where the computation divides by a largest or mean magnitude, that divisor is 1e-20 or more.
Results may differ from a plain program's by a relative error of at most 0.001.
Values may be sent and summed in bfloat16 or wider, within the bound.
A program may use at most 256 MiB of HBM per device.

v0:
```python
import functools

import jax
import jax.numpy as jnp
from jax import lax
from jax.experimental import pallas as pl
from jax.experimental.pallas import tpu as pltpu
from jax.sharding import PartitionSpec as P

LANES = 128
DEPTH = 4
MESH = pl.DeviceIdType.MESH


def kernel(n, owners, tile, w_ref, a_ref, rw_ref, gain_ref, out_ref, scale_ref, router_ref,
           w_buf, a_buf, staged, sums, parts, totals, routed,
           load_sem, own_sem, send_sem, recv_sem, sum_send, sum_recv, tot_send, tot_recv,
           row_send, row_recv, col_send, col_recv):
    me, mine = lax.axis_index("rows"), lax.axis_index("owner")
    experts, rows, cols = w_ref.shape
    block = rows // n
    piece = sums.shape[2]
    per_expert = rows // tile

    def peer(k):
        out, bit = 0, 1
        while bit < n:
            out = out + bit * (((me // bit) % 2 + (k // bit) % 2) % 2)
            bit *= 2
        return out

    def each_peer(fn):
        @pl.loop(1, n)
        def _(k):
            fn(peer(k))

    def each_owner(fn):
        @pl.loop(1, owners)
        def _(k):
            fn((mine + k) % owners)

    barrier = pltpu.get_barrier_semaphore()
    each_peer(lambda p: pl.semaphore_signal(barrier, inc=1, device_id={"rows": p}, device_id_type=MESH))
    each_owner(lambda q: pl.semaphore_signal(barrier, inc=1, device_id={"owner": q}, device_id_type=MESH))

    def loads(first, step):
        slot = step % DEPTH
        e = first + step // per_expert
        span = pl.ds(pl.multiple_of((step % per_expert) * tile, tile), tile)
        return (pltpu.make_async_copy(w_ref.at[e, span], w_buf.at[slot], load_sem.at[0, slot]),
                pltpu.make_async_copy(a_ref.at[e, span], a_buf.at[slot], load_sem.at[1, slot]))

    def prime(first):
        for step in range(DEPTH - 1):
            for copy in loads(first, step):
                copy.start()

    def stream(first, last, body):
        count = (last - first) * per_expert

        @pl.loop(0, count)
        def _(step):
            for copy in loads(first, step):
                copy.wait()

            @pl.when(step + (DEPTH - 1) < count)
            def _():
                for copy in loads(first, step + (DEPTH - 1)):
                    copy.start()

            body(first + step // per_expert, step % per_expert, step % DEPTH)

    def add_up(e, i, slot):
        for j in range(tile // LANES):
            span = slice(j * LANES, (j + 1) * LANES)
            acc = None
            for c in range(0, cols, LANES):
                f = jnp.abs(w_buf[slot, span, c:c + LANES] + a_buf[slot, span, c:c + LANES].astype(jnp.float32))
                acc = f if acc is None else acc + f
            at = i * (tile // LANES) + j
            sums[at // piece, e, pl.ds(at % piece, 1), :] = jnp.sum(acc.T, axis=0, keepdims=True)

    def narrow(e, i, slot):
        for j in range(tile // LANES):
            span = slice(j * LANES, (j + 1) * LANES)
            at = i * (tile // LANES) + j
            inverse = 1.0 / totals[at // piece, e, pl.ds(at % piece, 1), :]
            factor = jnp.broadcast_to(inverse, (LANES, LANES)).T
            where = pl.ds(pl.multiple_of(i * tile + j * LANES, LANES), LANES)
            for c in range(0, cols, LANES):
                f = w_buf[slot, span, c:c + LANES] + a_buf[slot, span, c:c + LANES].astype(jnp.float32)
                staged[e, where, c:c + LANES] = (f * factor).astype(jnp.bfloat16)

    def sum_copy(g, span, p, source):
        return pltpu.make_async_remote_copy(
            src_ref=sums.at[p, span], dst_ref=parts.at[source, span],
            send_sem=sum_send.at[g, p], recv_sem=sum_recv.at[g, source],
            device_id={"rows": p}, device_id_type=MESH)

    def total_copy(g, span, p, source):
        return pltpu.make_async_remote_copy(
            src_ref=totals.at[source, span], dst_ref=totals.at[source, span],
            send_sem=tot_send.at[g, p], recv_sem=tot_recv.at[g, source],
            device_id={"rows": p}, device_id_type=MESH)

    def exchange(g, first, last):
        span = pl.ds(first, last - first)
        each_peer(lambda p: sum_copy(g, span, p, me).start())
        parts[me, first:last] = sums[me, first:last]
        each_peer(lambda p: sum_copy(g, span, p, p).wait_recv())
        total = parts[0, first:last]
        for r in range(1, n):
            total = total + parts[r, first:last]
        totals[me, first:last] = total / (cols * n)
        each_peer(lambda p: total_copy(g, span, p, me).start())
        each_peer(lambda p: total_copy(g, span, p, p).wait_recv())

    def block_copy(e, p, source):
        return pltpu.make_async_remote_copy(
            src_ref=staged.at[e, pl.ds(pl.multiple_of(p * block, 16), block)],
            dst_ref=out_ref.at[e, :, pl.ds(pl.multiple_of(source * cols, LANES), cols)],
            send_sem=send_sem.at[e, p], recv_sem=recv_sem.at[e, source],
            device_id={"rows": p}, device_id_type=MESH)

    def own_copy(e):
        return pltpu.make_async_copy(
            staged.at[e, pl.ds(pl.multiple_of(me * block, 16), block)],
            out_ref.at[e, :, pl.ds(pl.multiple_of(me * cols, LANES), cols)],
            own_sem.at[e])

    def row_copy(p, source):
        return pltpu.make_async_remote_copy(
            src_ref=routed.at[mine, source], dst_ref=routed.at[mine, source],
            send_sem=row_send.at[p], recv_sem=row_recv.at[source],
            device_id={"rows": p}, device_id_type=MESH)

    def col_copy(q, source):
        return pltpu.make_async_remote_copy(
            src_ref=routed.at[source], dst_ref=routed.at[source],
            send_sem=col_send.at[q], recv_sem=col_recv.at[source],
            device_id={"owner": q}, device_id_type=MESH)

    prime(0)
    sums[...] = jnp.zeros_like(sums)
    routed[mine, me] = (rw_ref[...] * gain_ref[...]).astype(jnp.bfloat16)
    stream(0, 1, add_up)
    prime(0)
    pl.semaphore_wait(barrier, n - 1 + owners - 1)

    exchange(0, 0, 1)
    stream(0, 1, narrow)
    early = n // 2
    block_copy(0, peer(early), me).start()
    if experts > 1:
        prime(1)
    each_peer(lambda p: row_copy(p, me).start())
    own_copy(0).start()

    if experts > 1:
        stream(1, experts, add_up)
        prime(1)
        exchange(1, 1, experts)

    @pl.loop(1, n - 1)
    def _(k):
        block_copy(0, peer(k + k // early), me).start()

    each_peer(lambda p: row_copy(p, p).wait_recv())
    each_owner(lambda q: col_copy(q, mine).start())

    for e in range(1, experts):
        stream(e, e + 1, narrow)
        if e + 1 < experts:
            prime(e + 1)
        each_peer(lambda p, e=e: block_copy(e, p, me).start())
        own_copy(e).start()

    each_owner(lambda q: col_copy(q, q).wait_recv())
    scale_ref[...] = totals[...]
    router_ref[...] = routed[...]

    each_owner(lambda q: col_copy(q, mine).wait_send())
    each_peer(lambda p: row_copy(p, me).wait_send())
    for g, (first, last) in enumerate([(0, 1), (1, experts)][:min(experts, 2)]):
        span = pl.ds(first, last - first)
        each_peer(lambda p, g=g, span=span: sum_copy(g, span, p, me).wait_send())
        each_peer(lambda p, g=g, span=span: total_copy(g, span, p, me).wait_send())
    for e in range(experts):
        own_copy(e).wait()
        each_peer(lambda p, e=e: block_copy(e, p, me).wait_send())
        each_peer(lambda p, e=e: block_copy(e, p, p).wait_recv())


def with_kernel(n, owners, w_down, avg_down, router_weight, router_gain):
    experts, rows, cols = w_down.shape
    lane_rows = rows // LANES
    tile = LANES * max(t for t in range(1, 6) if lane_rows % t == 0)
    piece = -(-lane_rows // n)
    few = router_weight.shape[1]
    block = rows // n
    pair = pltpu.SemaphoreType.DMA((2, n))
    out, totals, routed = pl.pallas_call(
        functools.partial(kernel, n, owners, tile),
        out_shape=(
            jax.ShapeDtypeStruct((experts, block, cols * n), jnp.bfloat16),
            jax.ShapeDtypeStruct((n, experts, piece, LANES), jnp.float32),
            jax.ShapeDtypeStruct((owners, n, few, cols), jnp.bfloat16),
        ),
        in_specs=[pl.BlockSpec(memory_space=pl.ANY)] * 2 + [pl.BlockSpec(memory_space=pltpu.VMEM)] * 2,
        out_specs=(
            pl.BlockSpec(memory_space=pl.ANY),
            pl.BlockSpec(memory_space=pltpu.VMEM),
            pl.BlockSpec(memory_space=pltpu.VMEM),
        ),
        scratch_shapes=[
            pltpu.VMEM((DEPTH, tile, cols), jnp.float32),
            pltpu.VMEM((DEPTH, tile, cols), jnp.bfloat16),
            pltpu.VMEM((experts, rows, cols), jnp.bfloat16),
            pltpu.VMEM((n, experts, piece, LANES), jnp.float32),
            pltpu.VMEM((n, experts, piece, LANES), jnp.float32),
            pltpu.VMEM((n, experts, piece, LANES), jnp.float32),
            pltpu.VMEM((owners, n, few, cols), jnp.bfloat16),
            pltpu.SemaphoreType.DMA((2, DEPTH)),
            pltpu.SemaphoreType.DMA((experts,)),
            pltpu.SemaphoreType.DMA((experts, n)),
            pltpu.SemaphoreType.DMA((experts, n)),
            pair, pair, pair, pair,
            pltpu.SemaphoreType.DMA((n,)),
            pltpu.SemaphoreType.DMA((n,)),
            pltpu.SemaphoreType.DMA((owners,)),
            pltpu.SemaphoreType.DMA((owners,)),
        ],
        compiler_params=pltpu.CompilerParams(
            collective_id=0, has_side_effects=True, vmem_limit_bytes=60000 * 1024
        ),
        name="serve",
    )(w_down, avg_down, router_weight.T, router_gain[None, :])
    scales = jnp.transpose(totals, (1, 0, 2, 3)).reshape(experts, -1)
    scales = lax.dynamic_slice_in_dim(scales, lax.axis_index("rows") * block, block, axis=1)
    router = jnp.transpose(routed, (0, 2, 1, 3)).reshape(owners * few, n * cols).T
    return out, scales, router


def with_collectives(n, owners, w_down, avg_down, router_weight, router_gain):
    fresh = w_down + avg_down.astype(jnp.float32)
    scales = lax.psum(jnp.sum(jnp.abs(fresh), axis=2), "rows") / (w_down.shape[2] * n)
    narrow = (fresh / jnp.expand_dims(scales, 2)).astype(jnp.bfloat16)
    out = lax.all_to_all(narrow, "rows", split_axis=1, concat_axis=2, tiled=True)
    scales = lax.dynamic_slice_in_dim(scales, lax.axis_index("rows") * out.shape[1], out.shape[1], axis=1)
    part = (router_weight * router_gain[:, None]).astype(jnp.bfloat16)
    router = lax.all_gather(lax.all_gather(part, "rows", axis=0, tiled=True), "owner", axis=1, tiled=True)
    return out, scales, router


def solution(mesh):
    n, owners = mesh.shape["rows"], mesh.shape["owner"]

    def per_device(w_down, avg_down, router_weight, router_gain):
        experts, rows, cols = w_down.shape
        fits = (n & (n - 1)) == 0 and rows % LANES == 0 and rows % (16 * n) == 0 and cols % LANES == 0
        path = with_kernel if fits else with_collectives
        return path(n, owners, w_down, avg_down, router_weight, router_gain)

    return jax.shard_map(
        per_device,
        mesh=mesh,
        in_specs=(
            P("owner", None, "rows"),
            P("owner", None, "rows"),
            P("rows", "owner"),
            P("rows"),
        ),
        out_specs=(P("owner", "rows", None), P("owner", "rows"), P()),
        check_vma=False,
    )
```

profile of v0, /device:TPU:8, one launch (start us, length us, event | category | flops | bytes accessed | tf_op | source)
XLA Modules:
  0.0 619.2 jit_solution(5191970275881480512)
XLA Ops:
  0.6 597.3 %serve.1 = (bf16[4,800,4096]{2,1,0:T(8,128)(2,1)}, f32[8,4,7,128]{3,2,1,0:T(8,128)}, bf16[4,8,4,512]{3,2,1,0:T(4,128)(2,1)}) custom-call(f32[4,6400,512]{2,1,0:T(8,128)} %w_ref.1, bf16[4,6400,512]{2,1,0:T(8,128)(2,1)} %a_ref.1, f32[4,512]{1,0:T(4,128)} %bitcast.13, f32[1,512]{1,0:T(1,128)} %bitcast.14), custom_call_target="tpu_custom_call" | custom-call | tf_op jit(solution)/shard_map/serve/pallas_call | solution.py:202
  598.0 0.9 copy.7
  598.9 0.7 constant_dynamic-slice_fusion
  599.6 0.9 copy.8
  600.5 0.7 copy.9
  601.2 17.9 %copy.11 = bf16[4,800,4096]{2,1,0:T(8,128)(2,1)} copy(bf16[4,800,4096]{2,1,0:T(8,128)(2,1)} %get-tuple-element.12) | data formatting | bytes 52428800
  (1 shorter events, 0.0 us)
where the time goes:
time: 619 us
  Pallas kernels  597 us (96%)
  local copies, waits for them, and re-layouts  21.2 us (3%)
    pallas_call x1, Pallas kernels, with_kernel(): pl.pallas_call(functools.partial(kernel, n, owners, tile), out_shape=(jax...  597 us
    unnamed x2, local copies, waits for them, and re-layouts  18.6 us

commit v1 on v0

v1 whole, which is shorter than its diff:
```python
import functools

import jax
import jax.numpy as jnp
from jax import lax
from jax.experimental import pallas as pl
from jax.experimental.pallas import tpu as pltpu
from jax.sharding import PartitionSpec as P

LANES = 128
DEPTH = 4
VMEM_LIMIT = 38 * 1024 * 1024
MESH = pl.DeviceIdType.MESH


def pieces(low, high):
    return [(at // LANES, at, min(LANES, high - at)) for at in range(low, high, LANES)]


def kernel(n, owners, first, w_ref, a_ref, rw_ref, gain_ref, out_ref, totals, totals0, routed,
           w_buf, a_buf, staged, sums, parts, halves, sums0, parts0,
           load_sem, load0_sem, send_sem, recv_sem, sum0_send, sum0_recv,
           part_send, part_recv, half_send, half_recv, tot_send, tot_recv,
           row_send, row_recv, col_send, col_recv):
    me, mine = lax.axis_index("rows"), lax.axis_index("owner")
    experts, rows, cols = w_ref.shape
    block = rows // n
    half, quarter = n // 2, n // 4
    side, place = me // half, me % quarter
    outer = (me // quarter) % 2 == side
    inner = (me // quarter) % 2 != side
    groups = [(0, first, block)] + [(e, 0, block) for e in range(1, experts)]
    spans = [(0, 0, first)] + groups

    def peer(k):
        out, bit = 0, 1
        while bit < n:
            out = out + bit * (((me // bit) % 2 + (k // bit) % 2) % 2)
            bit *= 2
        return out

    def each_peer(fn):
        @pl.loop(1, n)
        def _(k):
            fn(peer(k))

    def each_owner(fn):
        @pl.loop(1, owners)
        def _(k):
            fn((mine + k) % owners)

    def each_outer(fn):
        @pl.loop(0, quarter)
        def _(i):
            p = side * (half + quarter) + i
            pl.when(p != me)(lambda: fn(p))

    def each_beside(fn):
        @pl.loop(1, half)
        def _(k):
            fn(peer(k))

    barrier = pltpu.get_barrier_semaphore()
    each_peer(lambda p: pl.semaphore_signal(barrier, inc=1, device_id={"rows": p}, device_id_type=MESH))
    each_owner(lambda q: pl.semaphore_signal(barrier, inc=1, device_id={"owner": q}, device_id_type=MESH))

    def rows_of(p, low, count):
        return pl.ds(pl.multiple_of(p * block + low, 16), count)

    def first_loads(k):
        span = rows_of(peer(k), 0, first)
        to = pl.ds(pl.multiple_of((k % 2) * first, LANES), first)
        return (pltpu.make_async_copy(w_ref.at[0, span], w_buf.at[k // 2, to], load0_sem.at[0, k]),
                pltpu.make_async_copy(a_ref.at[0, span], a_buf.at[k // 2, to], load0_sem.at[1, k]))

    def loads(e, low, high, step):
        slot, span, to = step % DEPTH, rows_of(peer(order(step)), low, high - low), pl.ds(0, high - low)
        return (pltpu.make_async_copy(w_ref.at[e, span], w_buf.at[slot, to], load_sem.at[0, slot]),
                pltpu.make_async_copy(a_ref.at[e, span], a_buf.at[slot, to], load_sem.at[1, slot]))

    def order(step):
        return (step + half) % n

    def prime(group):
        for step in range(min(DEPTH - 1, n)):
            for copy in loads(*group, step):
                copy.start()

    def stream(group, body):
        @pl.loop(0, n)
        def _(step):
            for copy in loads(*group, step):
                copy.wait()

            @pl.when(step + (DEPTH - 1) < n)
            def _():
                for copy in loads(*group, step + (DEPTH - 1)):
                    copy.start()

            body(order(step), step)

    def fresh(slot, span, c):
        return w_buf[slot, span, c:c + LANES] + a_buf[slot, span, c:c + LANES].astype(jnp.float32)

    def row_sums(slot, span):
        acc = None
        for c in range(0, cols, LANES):
            f = jnp.abs(fresh(slot, span, c))
            acc = f if acc is None else acc + f
        return jnp.sum(acc.T, axis=0, keepdims=True)

    def narrow(e, low, high, k, slot, start, total):
        p = peer(k)

        def write(put):
            for j, at, size in pieces(low, high):
                factor = jnp.broadcast_to(1.0 / total(p, j), (LANES, LANES)).T[:size]
                span = pl.ds(pl.multiple_of(start + (at - low), LANES), size)
                for c in range(0, cols, LANES):
                    put(at, size, c, (fresh(slot, span, c) * factor).astype(jnp.bfloat16))

        def keep(at, size, c, value):
            out_ref[e, at:at + size, pl.ds(pl.multiple_of(me * cols + c, LANES), LANES)] = value

        def stage(at, size, c, value):
            staged[e, rows_of(p, at, size), c:c + LANES] = value

        pl.when(k == 0)(lambda: write(keep))
        pl.when(k != 0)(lambda: write(stage))

    def block_copy(part, p, source):
        e, low, high = spans[part]
        return pltpu.make_async_remote_copy(
            src_ref=staged.at[e, rows_of(p, low, high - low)],
            dst_ref=out_ref.at[e, pl.ds(low, high - low), pl.ds(pl.multiple_of(source * cols, LANES), cols)],
            send_sem=send_sem.at[part, p], recv_sem=recv_sem.at[part, source],
            device_id={"rows": p}, device_id_type=MESH)

    def first_copy(p, source):
        return pltpu.make_async_remote_copy(
            src_ref=sums0, dst_ref=parts0.at[source],
            send_sem=sum0_send.at[p], recv_sem=sum0_recv.at[source],
            device_id={"rows": p}, device_id_type=MESH)

    def part_copy(g, p, source):
        e = groups[g][0]
        return pltpu.make_async_remote_copy(
            src_ref=sums.at[:, p % quarter, e], dst_ref=parts.at[source % half, :, e],
            send_sem=part_send.at[g, p % quarter], recv_sem=part_recv.at[g, source % half],
            device_id={"rows": p}, device_id_type=MESH)

    def half_copy(g):
        e = groups[g][0]
        return pltpu.make_async_remote_copy(
            src_ref=halves.at[0, :, e], dst_ref=halves.at[1, :, e],
            send_sem=half_send.at[g], recv_sem=half_recv.at[g],
            device_id={"rows": peer(half + quarter)}, device_id_type=MESH)

    def total_copy(g, p, source):
        e, at = groups[g][0], source % quarter
        return pltpu.make_async_remote_copy(
            src_ref=totals.at[:, at, e], dst_ref=totals.at[:, at, e],
            send_sem=tot_send.at[g, p % half], recv_sem=tot_recv.at[g, at],
            device_id={"rows": p}, device_id_type=MESH)

    def send_sums(g):
        each_outer(lambda p: part_copy(g, p, me).start())

    def cross_sums(g):
        @pl.when(outer)
        def _():
            e = groups[g][0]
            parts[me % half, :, e] = sums[:, place, e]
            each_beside(lambda p: part_copy(g, p, p).wait_recv())
            total = parts[0, :, e]
            for r in range(1, half):
                total = total + parts[r, :, e]
            halves[0, :, e] = total
            half_copy(g).start()

    def send_totals(g):
        @pl.when(outer)
        def _():
            e = groups[g][0]
            half_copy(g).wait_recv()
            totals[:, place, e] = (halves[0, :, e] + halves[1, :, e]) / (cols * n)
            each_beside(lambda p: total_copy(g, p, me).start())

    def take_totals(g):
        each_outer(lambda p: total_copy(g, p, p).wait_recv())

    def row_copy(p, source):
        return pltpu.make_async_remote_copy(
            src_ref=routed.at[mine, source], dst_ref=routed.at[mine, source],
            send_sem=row_send.at[p], recv_sem=row_recv.at[source],
            device_id={"rows": p}, device_id_type=MESH)

    def col_copy(q, source):
        return pltpu.make_async_remote_copy(
            src_ref=routed.at[source], dst_ref=routed.at[source],
            send_sem=col_send.at[q], recv_sem=col_recv.at[source],
            device_id={"owner": q}, device_id_type=MESH)

    def send_crossing(part, k):
        @pl.when(inner & (k >= half))
        def _():
            block_copy(part, peer(k), me).start()

    @pl.loop(0, n)
    def _(k):
        for copy in first_loads(k):
            copy.start()

    sums[...] = jnp.zeros_like(sums)
    routed[mine, me] = (rw_ref[...] * gain_ref[...]).astype(jnp.bfloat16)

    @pl.loop(0, n)
    def _(k):
        for copy in first_loads(k):
            copy.wait()
        for j, at, size in pieces(0, first):
            span = pl.ds(pl.multiple_of((k % 2) * first + at, LANES), size)
            sums0[j, pl.ds(peer(k), 1), :] = row_sums(k // 2, span)

    pl.semaphore_wait(barrier, n - 1 + owners - 1)
    each_peer(lambda p: first_copy(p, me).start())
    parts0[me] = sums0[...]
    each_peer(lambda p: row_copy(p, me).start())
    each_peer(lambda p: first_copy(p, p).wait_recv())
    total = parts0[0]
    for r in range(1, n):
        total = total + parts0[r]
    totals0[...] = total / (cols * n)

    @pl.loop(0, n)
    def _(step):
        k = order(step)
        narrow(0, 0, first, k, k // 2, (k % 2) * first, lambda p, j: totals0[j, pl.ds(p, 1), :])
        send_crossing(0, k)

    def add_up(g, behind):
        e, low, high = groups[g]

        def body(k, step):
            p = peer(k)
            for j, at, size in pieces(low, high):
                sums[p // quarter, p % quarter, e, j:j + 1, 0:size] = row_sums(step % DEPTH, pl.ds(at - low, size))
            if behind is not None:
                pl.when(step == n // 2 - 1)(lambda: cross_sums(behind))
                pl.when(step == n - 1)(lambda: send_totals(behind))

        stream(groups[g], body)

    def narrow_all(g):
        e, low, high = groups[g]

        def body(k, step):
            narrow(e, low, high, k, step % DEPTH, 0,
                   lambda p, j: totals[p // quarter, p % quarter, e, j:j + 1, :])
            send_crossing(g + 1, k)

        stream(groups[g], body)

    prime(groups[0])
    add_up(0, None)
    for g in range(experts):
        send_sums(g)
        if g + 1 < experts:
            prime(groups[g + 1])
            add_up(g + 1, g)
        else:
            cross_sums(g)
            send_totals(g)
        prime(groups[g])
        take_totals(g)
        narrow_all(g)

    for part in range(experts + 1):
        each_beside(lambda p, part=part: block_copy(part, p, me).start())

    each_peer(lambda p: row_copy(p, p).wait_recv())
    each_owner(lambda q: col_copy(q, mine).start())

    @pl.when(outer)
    def _():
        for part in range(experts + 1):
            @pl.loop(half, n)
            def _(k, part=part):
                block_copy(part, peer(k), me).start()

    each_owner(lambda q: col_copy(q, q).wait_recv())
    each_owner(lambda q: col_copy(q, mine).wait_send())
    each_peer(lambda p: row_copy(p, me).wait_send())
    each_peer(lambda p: first_copy(p, me).wait_send())
    for g in range(experts):
        each_outer(lambda p, g=g: part_copy(g, p, me).wait_send())

        @pl.when(outer)
        def _(g=g):
            half_copy(g).wait_send()
            each_beside(lambda p: total_copy(g, p, me).wait_send())
    for part in range(experts + 1):
        each_peer(lambda p, part=part: block_copy(part, p, me).wait_send())
        each_peer(lambda p, part=part: block_copy(part, p, p).wait_recv())


def finish(first, held, totals, totals0, routed, out_ref, scale_ref, router_ref, scale, wide, router, out_sem, sem):
    me = lax.axis_index("rows")
    experts, block, _ = held.shape
    owners, n, few, cols = routed.shape
    quarter = totals.shape[1]
    outs = [pltpu.make_async_copy(held.at[e], out_ref.at[e], out_sem.at[e]) for e in range(experts)]
    for copy in outs:
        copy.start()
    for e in range(experts):
        for j, at, size in pieces(0, block):
            if e == 0 and at < first:
                row = totals0[j, pl.ds(me, 1), :]
            else:
                row = totals[me // quarter, me % quarter, e, j:j + 1, 0:size]
            scale[e:e + 1, at:at + size] = row
    for q in range(owners):
        for r in range(n):
            wide[q * few:(q + 1) * few, r * cols:(r + 1) * cols] = routed[q, r].astype(jnp.float32)
    router[...] = wide[...].astype(jnp.bfloat16)
    small = [pltpu.make_async_copy(scale, scale_ref, sem.at[0]), pltpu.make_async_copy(router, router_ref, sem.at[1])]
    for copy in small:
        copy.start()
    for copy in small + outs:
        copy.wait()


def with_kernel(n, owners, w_down, avg_down, router_weight, router_gain):
    experts, rows, cols = w_down.shape
    few = router_weight.shape[1]
    block = rows // n
    half, quarter = n // 2, n // 4
    piece = -(-block // LANES)
    first = LANES * min(2, (block - 1) // LANES)
    dma = pltpu.SemaphoreType.DMA
    anywhere, vmem = pl.BlockSpec(memory_space=pl.ANY), pl.BlockSpec(memory_space=pltpu.VMEM)
    sums = pltpu.VMEM((4, quarter, experts, piece, LANES), jnp.float32)
    sums0 = pltpu.VMEM((first // LANES, n, LANES), jnp.float32)
    held = pl.pallas_call(
        functools.partial(kernel, n, owners, first),
        out_shape=(
            pltpu.VMEM((experts, block, cols * n), jnp.bfloat16),
            sums,
            sums0,
            pltpu.VMEM((owners, n, few, cols), jnp.bfloat16),
        ),
        in_specs=[anywhere] * 2 + [vmem] * 2,
        out_specs=(vmem,) * 4,
        scratch_shapes=[
            pltpu.VMEM((DEPTH, block, cols), jnp.float32),
            pltpu.VMEM((DEPTH, block, cols), jnp.bfloat16),
            pltpu.VMEM((experts, rows, cols), jnp.bfloat16),
            sums,
            pltpu.VMEM((half, 4, experts, piece, LANES), jnp.float32),
            pltpu.VMEM((2, 4, experts, piece, LANES), jnp.float32),
            sums0,
            pltpu.VMEM((n, first // LANES, n, LANES), jnp.float32),
            dma((2, DEPTH)), dma((2, n)),
            dma((experts + 1, n)), dma((experts + 1, n)),
            dma((n,)), dma((n,)),
            dma((experts, quarter)), dma((experts, half)), dma((experts,)), dma((experts,)),
            dma((experts, half)), dma((experts, quarter)),
            dma((n,)), dma((n,)), dma((owners,)), dma((owners,)),
        ],
        compiler_params=pltpu.CompilerParams(
            collective_id=0, has_side_effects=True, vmem_limit_bytes=VMEM_LIMIT
        ),
        name="serve",
    )(w_down, avg_down, router_weight.T, router_gain[None, :])
    out, scales, router = pl.pallas_call(
        functools.partial(finish, first),
        out_shape=(
            jax.ShapeDtypeStruct((experts, block, cols * n), jnp.bfloat16),
            jax.ShapeDtypeStruct((experts, block), jnp.float32),
            jax.ShapeDtypeStruct((owners * few, cols * n), jnp.bfloat16),
        ),
        in_specs=[vmem] * 4,
        out_specs=(anywhere,) * 3,
        scratch_shapes=[
            pltpu.VMEM((experts, block), jnp.float32),
            pltpu.VMEM((owners * few, cols * n), jnp.float32),
            pltpu.VMEM((owners * few, cols * n), jnp.bfloat16),
            dma((experts,)), dma((2,)),
        ],
        compiler_params=pltpu.CompilerParams(vmem_limit_bytes=4 * 1024 * 1024),
        name="finish",
    )(*held)
    return out, scales, router.T


def with_collectives(n, owners, w_down, avg_down, router_weight, router_gain):
    fresh = w_down + avg_down.astype(jnp.float32)
    scales = lax.psum(jnp.sum(jnp.abs(fresh), axis=2), "rows") / (w_down.shape[2] * n)
    narrow = (fresh / jnp.expand_dims(scales, 2)).astype(jnp.bfloat16)
    out = lax.all_to_all(narrow, "rows", split_axis=1, concat_axis=2, tiled=True)
    scales = lax.dynamic_slice_in_dim(scales, lax.axis_index("rows") * out.shape[1], out.shape[1], axis=1)
    part = (router_weight * router_gain[:, None]).astype(jnp.bfloat16)
    router = lax.all_gather(lax.all_gather(part, "rows", axis=0, tiled=True), "owner", axis=1, tiled=True)
    return out, scales, router


def solution(mesh):
    n, owners = mesh.shape["rows"], mesh.shape["owner"]

    def per_device(w_down, avg_down, router_weight, router_gain):
        experts, rows, cols = w_down.shape
        fits = n >= 4 and (n & (n - 1)) == 0 and rows // n > LANES and rows % LANES == 0 and rows % (16 * n) == 0 and cols % LANES == 0
        path = with_kernel if fits else with_collectives
        return path(n, owners, w_down, avg_down, router_weight, router_gain)

    return jax.shard_map(
        per_device,
        mesh=mesh,
        in_specs=(
            P("owner", None, "rows"),
            P("owner", None, "rows"),
            P("rows", "owner"),
            P("rows"),
        ),
        out_specs=(P("owner", "rows", None), P("owner", "rows"), P()),
        check_vma=False,
    )
```

time: 619 us -> 593 us (0.958)
  local copies, waits for them, and re-layouts: 21.2 us -> 0 us
    unnamed x2 -> x0, local copies, waits for them, and re-layouts: 18.6 us -> none
    pallas_call x1 -> x2, Pallas kernels: 597 us -> 592 us  [the longest x1 583 us: with_kernel(): pl.pallas_call(functools.partial(kernel, n, owners, first), out_shape=(pl...]
where the time goes in v1:
time: 593 us
  Pallas kernels  592 us (100%)
    pallas_call x1, Pallas kernels, with_kernel(): pl.pallas_call(functools.partial(kernel, n, owners, first), out_shape=(pl...  583 us

profile of v1, /device:TPU:8, one launch (start us, length us, event | category | flops | bytes accessed | tf_op | source)
XLA Modules:
  0.0 592.7 jit_solution(14206274727794237138)
XLA Ops:
  0.6 583.1 %serve.1 = (bf16[4,800,4096]{2,1,0:T(8,128)(2,1)S(1)}, f32[4,2,4,7,128]{4,3,2,1,0:T(8,128)S(1)}, f32[2,8,128]{2,1,0:T(8,128)S(1)}, bf16[4,8,4,512]{3,2,1,0:T(4,128)(2,1)S(1)}) custom-call(f32[4,6400,512]{2,1,0:T(8,128)} %w_ref.1, bf16[4,6400,512]{2,1,0:T(8,128)(2,1)} %a_ref.1, f32[4,512]{1,0:T(4,128)} %bitcast.3, f32[1,512]{1,0:T(1,128)} %bitcast.4), custom_call_target="tpu_custom_call" | custom-call | tf_op jit(solution)/shard_map/serve/pallas_call | solution.py:344
  583.8 8.9 %finish.1 = (bf16[4,800,4096]{2,1,0:T(8,128)(2,1)}, f32[4,800]{1,0:T(4,128)}, bf16[16,4096]{1,0:T(8,128)(2,1)}) custom-call(bf16[4,800,4096]{2,1,0:T(8,128)(2,1)S(1)} %get-tuple-element.10.held, f32[4,2,4,7,128]{4,3,2,1,0:T(8,128)S(1)} %get-tuple-element.11.totals, f32[2,8,128]{2,1,0:T(8,128)S(1)} %get-tuple-element.12.totals0, ...), custom_call_target="tpu_custom_call" | custom-call | tf_op jit(solution)/shard_map/finish/pallas_call | solution.py:375

commit v2 on v1

--- a/solution.py
+++ b/solution.py
@@ -29,6 +29,7 @@
     side, place = me // half, me % quarter
     outer = (me // quarter) % 2 == side
     inner = (me // quarter) % 2 != side
+    turn = (mine % 2) * quarter
     groups = [(0, first, block)] + [(e, 0, block) for e in range(1, experts)]
     spans = [(0, 0, first)] + groups
 
@@ -79,7 +80,7 @@
                 pltpu.make_async_copy(a_ref.at[e, span], a_buf.at[slot, to], load_sem.at[1, slot]))
 
     def order(step):
-        return (step + half) % n
+        return jnp.where(step < half, half + (step + turn) % half, step - half)
 
     def prime(group):
         for step in range(min(DEPTH - 1, n)):
@@ -202,9 +203,15 @@
             device_id={"owner": q}, device_id_type=MESH)
 
     def send_crossing(part, k):
-        @pl.when(inner & (k >= half))
+        @pl.when(inner & (k >= half) & ((k - half) // quarter == mine % 2 if part else True))
         def _():
             block_copy(part, peer(k), me).start()
+
+    def send_late(parts, low, high):
+        for part in parts:
+            @pl.loop(low, high)
+            def _(k, part=part):
+                block_copy(part, peer(k), me).start()
 
     @pl.loop(0, n)
     def _(k):
@@ -275,18 +282,19 @@
         take_totals(g)
         narrow_all(g)
 
-    for part in range(experts + 1):
-        each_beside(lambda p, part=part: block_copy(part, p, me).start())
+    @pl.when(inner)
+    def _():
+        send_late(range(1, experts + 1), half + quarter - turn, n - turn)
+
+    send_late(range(experts + 1), 1, half)
 
     each_peer(lambda p: row_copy(p, p).wait_recv())
     each_owner(lambda q: col_copy(q, mine).start())
 
     @pl.when(outer)
     def _():
-        for part in range(experts + 1):
-            @pl.loop(half, n)
-            def _(k, part=part):
-                block_copy(part, peer(k), me).start()
+        send_late(range(experts + 1), half + turn, half + quarter + turn)
+        send_late(range(experts + 1), half + quarter - turn, n - turn)
 
     each_owner(lambda q: col_copy(q, q).wait_recv())
     each_owner(lambda q: col_copy(q, mine).wait_send())

time: 593 us -> 584 us (0.985)
  Pallas kernels: 592 us -> 583 us
    pallas_call x1, Pallas kernels: 583 us -> 575 us  [with_kernel(): pl.pallas_call(functools.partial(kernel, n, owners, first), out_shape=(pl...]
where the time goes in v2:
time: 584 us
  Pallas kernels  583 us (100%)
    pallas_call x1, Pallas kernels, with_kernel(): pl.pallas_call(functools.partial(kernel, n, owners, first), out_shape=(pl...  575 us

profile of v2, /device:TPU:8, one launch (start us, length us, event | category | flops | bytes accessed | tf_op | source)
XLA Modules:
  0.0 584.1 jit_solution(11130568828609501377)
XLA Ops:
  0.6 574.5 %serve.1 = (bf16[4,800,4096]{2,1,0:T(8,128)(2,1)S(1)}, f32[4,2,4,7,128]{4,3,2,1,0:T(8,128)S(1)}, f32[2,8,128]{2,1,0:T(8,128)S(1)}, bf16[4,8,4,512]{3,2,1,0:T(4,128)(2,1)S(1)}) custom-call(f32[4,6400,512]{2,1,0:T(8,128)} %w_ref.1, bf16[4,6400,512]{2,1,0:T(8,128)(2,1)} %a_ref.1, f32[4,512]{1,0:T(4,128)} %bitcast.3, f32[1,512]{1,0:T(1,128)} %bitcast.4), custom_call_target="tpu_custom_call" | custom-call | tf_op jit(solution)/shard_map/serve/pallas_call | solution.py:352
  575.2 8.9 %finish.1 = (bf16[4,800,4096]{2,1,0:T(8,128)(2,1)}, f32[4,800]{1,0:T(4,128)}, bf16[16,4096]{1,0:T(8,128)(2,1)}) custom-call(bf16[4,800,4096]{2,1,0:T(8,128)(2,1)S(1)} %get-tuple-element.10.held, f32[4,2,4,7,128]{4,3,2,1,0:T(8,128)S(1)} %get-tuple-element.11.totals, f32[2,8,128]{2,1,0:T(8,128)S(1)} %get-tuple-element.12.totals0, ...), custom_call_target="tpu_custom_call" | custom-call | tf_op jit(solution)/shard_map/finish/pallas_call | solution.py:383

commit v3 on v2

--- a/solution.py
+++ b/solution.py
@@ -9,7 +9,7 @@
 
 LANES = 128
 DEPTH = 4
-VMEM_LIMIT = 38 * 1024 * 1024
+VMEM_LIMIT = 36 * 1024 * 1024
 MESH = pl.DeviceIdType.MESH
 
 
@@ -17,11 +17,19 @@
     return [(at // LANES, at, min(LANES, high - at)) for at in range(low, high, LANES)]
 
 
-def kernel(n, owners, first, w_ref, a_ref, rw_ref, gain_ref, out_ref, totals, totals0, routed,
+def flipped(n, me, k):
+    out, bit = 0, 1
+    while bit < n:
+        out = out + bit * (((me // bit) % 2 + (k // bit) % 2) % 2)
+        bit *= 2
+    return out
+
+
+def kernel(n, owners, first, cuts, w_ref, a_ref, rw_ref, gain_ref, out_ref, totals, totals0, routed, kept,
            w_buf, a_buf, staged, sums, parts, halves, sums0, parts0,
            load_sem, load0_sem, send_sem, recv_sem, sum0_send, sum0_recv,
            part_send, part_recv, half_send, half_recv, tot_send, tot_recv,
-           row_send, row_recv, col_send, col_recv):
+           row_send, row_recv, col_send, col_recv, turn_sem):
     me, mine = lax.axis_index("rows"), lax.axis_index("owner")
     experts, rows, cols = w_ref.shape
     block = rows // n
@@ -31,14 +39,13 @@
     inner = (me // quarter) % 2 != side
     turn = (mine % 2) * quarter
     groups = [(0, first, block)] + [(e, 0, block) for e in range(1, experts)]
-    spans = [(0, 0, first)] + groups
+    e = experts - 1
+    last = experts + 3
+    spans = [(0, 0, first)] + groups[:-1] + [(e, low, high) for low, high in zip((groups[-1][1],) + cuts, cuts + (block,))]
+    parts_of = lambda g: range(experts, last + 1) if g == experts - 1 else [g + 1]
 
     def peer(k):
-        out, bit = 0, 1
-        while bit < n:
-            out = out + bit * (((me // bit) % 2 + (k // bit) % 2) % 2)
-            bit *= 2
-        return out
+        return flipped(n, me, k)
 
     def each_peer(fn):
         @pl.loop(1, n)
@@ -203,9 +210,12 @@
             device_id={"owner": q}, device_id_type=MESH)
 
     def send_crossing(part, k):
-        @pl.when(inner & (k >= half) & ((k - half) // quarter == mine % 2 if part else True))
+        @pl.when(inner & (k >= half) & (k < end(part)) & ((k - half) // quarter == mine % 2 if part else True))
         def _():
             block_copy(part, peer(k), me).start()
+
+    def end(part):
+        return half + quarter if part == last else n
 
     def send_late(parts, low, high):
         for part in parts:
@@ -264,7 +274,8 @@
         def body(k, step):
             narrow(e, low, high, k, step % DEPTH, 0,
                    lambda p, j: totals[p // quarter, p % quarter, e, j:j + 1, :])
-            send_crossing(g + 1, k)
+            for part in parts_of(g):
+                send_crossing(part, k)
 
         stream(groups[g], body)
 
@@ -282,21 +293,43 @@
         take_totals(g)
         narrow_all(g)
 
+    for i in range(quarter):
+        kept[i] = staged[experts - 1, rows_of(peer(half + quarter + i), cuts[2], block - cuts[2]), :]
+
     @pl.when(inner)
     def _():
-        send_late(range(1, experts + 1), half + quarter - turn, n - turn)
-
-    send_late(range(experts + 1), 1, half)
+        send_late([*range(1, last - 1)], half + quarter - turn, n - turn)
+        send_late([last], half + quarter - turn, half + quarter)
+        send_late([last - 1], half + quarter - turn, n - turn)
+
+    send_late(range(last + 1), 1, half)
 
     each_peer(lambda p: row_copy(p, p).wait_recv())
     each_owner(lambda q: col_copy(q, mine).start())
 
     @pl.when(outer)
     def _():
-        send_late(range(experts + 1), half + turn, half + quarter + turn)
-        send_late(range(experts + 1), half + quarter - turn, n - turn)
+        @pl.loop(0, 2)
+        def _(i):
+            begin = half + (quarter * i + turn) % half
+            send_late(range(last - 2), begin, begin + quarter)
+
+            @pl.when(begin == half)
+            def _():
+                send_late(range(last - 2, last + 1), half, half + quarter)
 
     each_owner(lambda q: col_copy(q, q).wait_recv())
+
+    @pl.when(inner)
+    def _():
+        block_copy(last - 1, peer(n - turn - 2), me).wait_send()
+        pl.semaphore_signal(turn_sem, inc=1, device_id={"rows": peer(quarter)}, device_id_type=MESH)
+
+    @pl.when(outer)
+    def _():
+        pl.semaphore_wait(turn_sem, 1)
+        send_late(range(last - 2, last + 1), half + quarter, n)
+
     each_owner(lambda q: col_copy(q, mine).wait_send())
     each_peer(lambda p: row_copy(p, me).wait_send())
     each_peer(lambda p: first_copy(p, me).wait_send())
@@ -307,12 +340,65 @@
         def _(g=g):
             half_copy(g).wait_send()
             each_beside(lambda p: total_copy(g, p, me).wait_send())
-    for part in range(experts + 1):
-        each_peer(lambda p, part=part: block_copy(part, p, me).wait_send())
-        each_peer(lambda p, part=part: block_copy(part, p, p).wait_recv())
-
-
-def finish(first, held, totals, totals0, routed, out_ref, scale_ref, router_ref, scale, wide, router, out_sem, sem):
+    for part in range(last + 1):
+        @pl.loop(1, n)
+        def _(k, part=part):
+            p = peer(k)
+
+            @pl.when(outer | (k < end(part)))
+            def _():
+                if part == last - 1:
+                    pl.when(outer | (k != n - turn - 2))(lambda: block_copy(part, p, me).wait_send())
+                else:
+                    block_copy(part, p, me).wait_send()
+                block_copy(part, p, p).wait_recv()
+
+
+def swap(n, after_ref, kept, got, send_sem, recv_sem):
+    me = lax.axis_index("rows")
+    half, quarter = n // 2, n // 4
+
+    def peer(k):
+        return flipped(n, me, k)
+
+    def copy(i):
+        return pltpu.make_async_remote_copy(
+            src_ref=kept.at[i], dst_ref=got.at[i], send_sem=send_sem.at[i], recv_sem=recv_sem.at[i],
+            device_id={"rows": peer(half + quarter + i)}, device_id_type=MESH)
+
+    @pl.when((me // quarter) % 2 != me // half)
+    def _():
+        barrier = pltpu.get_barrier_semaphore()
+        for i in range(quarter):
+            pl.semaphore_signal(barrier, inc=1, device_id={"rows": peer(half + quarter + i)}, device_id_type=MESH)
+        pl.semaphore_wait(barrier, quarter)
+        for i in range(quarter):
+            copy(i).start()
+        for i in range(quarter):
+            copy(i).wait()
+
+
+def place(n, low, out_in, got, out_ref, sem):
+    me = lax.axis_index("rows")
+    quarter = n // 4
+    experts, block, _ = out_ref.shape
+    cols = got.shape[2]
+
+    @pl.when((me // quarter) % 2 != me // (n // 2))
+    def _():
+        copies = []
+        for i in range(quarter):
+            source = flipped(n, me, n - quarter + i)
+            copies.append(pltpu.make_async_copy(
+                got.at[i], out_ref.at[experts - 1, pl.ds(low, block - low), pl.ds(pl.multiple_of(source * cols, LANES), cols)],
+                sem.at[i]))
+        for copy in copies:
+            copy.start()
+        for copy in copies:
+            copy.wait()
+
+
+def finish(first, held, totals, totals0, routed, out_ref, scale_ref, router_ref, done, scale, wide, router, out_sem, sem):
     me = lax.axis_index("rows")
     experts, block, _ = held.shape
     owners, n, few, cols = routed.shape
@@ -336,6 +422,7 @@
         copy.start()
     for copy in small + outs:
         copy.wait()
+    done[...] = jnp.zeros_like(done)
 
 
 def with_kernel(n, owners, w_down, avg_down, router_weight, router_gain):
@@ -345,20 +432,24 @@
     half, quarter = n // 2, n // 4
     piece = -(-block // LANES)
     first = LANES * min(2, (block - 1) // LANES)
+    middle = block // 2 // LANES * LANES
+    cuts = (middle - LANES, middle, middle + LANES)
+    tail = pltpu.VMEM((quarter, block - cuts[2], cols), jnp.bfloat16)
     dma = pltpu.SemaphoreType.DMA
     anywhere, vmem = pl.BlockSpec(memory_space=pl.ANY), pl.BlockSpec(memory_space=pltpu.VMEM)
     sums = pltpu.VMEM((4, quarter, experts, piece, LANES), jnp.float32)
     sums0 = pltpu.VMEM((first // LANES, n, LANES), jnp.float32)
-    held = pl.pallas_call(
-        functools.partial(kernel, n, owners, first),
+    *held, kept = pl.pallas_call(
+        functools.partial(kernel, n, owners, first, cuts),
         out_shape=(
             pltpu.VMEM((experts, block, cols * n), jnp.bfloat16),
             sums,
             sums0,
             pltpu.VMEM((owners, n, few, cols), jnp.bfloat16),
+            tail,
         ),
         in_specs=[anywhere] * 2 + [vmem] * 2,
-        out_specs=(vmem,) * 4,
+        out_specs=(vmem,) * 5,
         scratch_shapes=[
             pltpu.VMEM((DEPTH, block, cols), jnp.float32),
             pltpu.VMEM((DEPTH, block, cols), jnp.bfloat16),
@@ -369,26 +460,28 @@
             sums0,
             pltpu.VMEM((n, first // LANES, n, LANES), jnp.float32),
             dma((2, DEPTH)), dma((2, n)),
-            dma((experts + 1, n)), dma((experts + 1, n)),
+            dma((experts + 4, n)), dma((experts + 4, n)),
             dma((n,)), dma((n,)),
             dma((experts, quarter)), dma((experts, half)), dma((experts,)), dma((experts,)),
             dma((experts, half)), dma((experts, quarter)),
             dma((n,)), dma((n,)), dma((owners,)), dma((owners,)),
+            pltpu.SemaphoreType.REGULAR,
         ],
         compiler_params=pltpu.CompilerParams(
             collective_id=0, has_side_effects=True, vmem_limit_bytes=VMEM_LIMIT
         ),
         name="serve",
     )(w_down, avg_down, router_weight.T, router_gain[None, :])
-    out, scales, router = pl.pallas_call(
+    out, scales, router, done = pl.pallas_call(
         functools.partial(finish, first),
         out_shape=(
             jax.ShapeDtypeStruct((experts, block, cols * n), jnp.bfloat16),
             jax.ShapeDtypeStruct((experts, block), jnp.float32),
             jax.ShapeDtypeStruct((owners * few, cols * n), jnp.bfloat16),
+            pltpu.VMEM((8, LANES), jnp.float32),
         ),
         in_specs=[vmem] * 4,
-        out_specs=(anywhere,) * 3,
+        out_specs=(anywhere,) * 3 + (vmem,),
         scratch_shapes=[
             pltpu.VMEM((experts, block), jnp.float32),
             pltpu.VMEM((owners * few, cols * n), jnp.float32),
@@ -398,6 +491,27 @@
         compiler_params=pltpu.CompilerParams(vmem_limit_bytes=4 * 1024 * 1024),
         name="finish",
     )(*held)
+    got = pl.pallas_call(
+        functools.partial(swap, n),
+        out_shape=tail,
+        in_specs=[vmem, vmem],
+        out_specs=vmem,
+        scratch_shapes=[dma((quarter,)), dma((quarter,))],
+        compiler_params=pltpu.CompilerParams(
+            collective_id=1, has_side_effects=True, vmem_limit_bytes=1024 * 1024
+        ),
+        name="swap",
+    )(done, kept)
+    out = pl.pallas_call(
+        functools.partial(place, n, cuts[2]),
+        out_shape=jax.ShapeDtypeStruct(out.shape, out.dtype),
+        in_specs=[anywhere, vmem],
+        out_specs=anywhere,
+        scratch_shapes=[dma((quarter,))],
+        input_output_aliases={0: 0},
+        compiler_params=pltpu.CompilerParams(vmem_limit_bytes=1024 * 1024),
+        name="place",
+    )(out, got)
     return out, scales, router.T
 
 
@@ -417,7 +531,7 @@
 
     def per_device(w_down, avg_down, router_weight, router_gain):
         experts, rows, cols = w_down.shape
-        fits = n >= 4 and (n & (n - 1)) == 0 and rows // n > LANES and rows % LANES == 0 and rows % (16 * n) == 0 and cols % LANES == 0
+        fits = n >= 8 and (n & (n - 1)) == 0 and rows // n >= 4 * LANES and rows % LANES == 0 and rows % (16 * n) == 0 and cols % LANES == 0
         path = with_kernel if fits else with_collectives
         return path(n, owners, w_down, avg_down, router_weight, router_gain)
 

time: 584 us -> 576 us (0.986)
  Pallas kernels: 583 us -> 575 us
    pallas_call x1 -> x3, Pallas kernels: 575 us -> 566 us  [the longest x1 550 us: with_kernel(): pl.pallas_call(functools.partial(kernel, n, owners, first, cuts), out_sha...]
where the time goes in v3:
time: 576 us; the launch traced here: 575 us
  Pallas kernels  575 us (100%)
    pallas_call x1, Pallas kernels, with_kernel(): pl.pallas_call(functools.partial(kernel, n, owners, first, cuts), out_sha...  550 us
    pallas_call x1, Pallas kernels, with_kernel(): pl.pallas_call(functools.partial(swap, n), out_shape=tail, in_specs=[vmem...  14.5 us

profile of v3, /device:TPU:8, one launch (start us, length us, event | category | flops | bytes accessed | tf_op | source)
XLA Modules:
  0.0 575.4 jit_solution(18152921900065417941)
XLA Ops:
  0.6 550.5 %serve.1 = (bf16[4,800,4096]{2,1,0:T(8,128)(2,1)S(1)}, f32[4,2,4,7,128]{4,3,2,1,0:T(8,128)S(1)}, f32[2,8,128]{2,1,0:T(8,128)S(1)}, bf16[4,8,4,512]{3,2,1,0:T(4,128)(2,1)S(1)}, bf16[2,288,512]{2,1,0:T(8,128)(2,1)S(1)}) custom-call(f32[4,6400,512]{2,1,0:T(8,128)} %w_ref.1, bf16[4,6400,512]{2,1,0:T(8,128)(2,1)} %a_ref.1, f32[4,512]{1,0:T(4,128)} %bitcast.3, ...), custom_call_target="tpu_custom_call" | custom-call | tf_op jit(solution)/shard_map/serve/pallas_call | solution.py:442
  551.1 8.9 %finish.1 = (bf16[4,800,4096]{2,1,0:T(8,128)(2,1)}, f32[4,800]{1,0:T(4,128)}, bf16[16,4096]{1,0:T(8,128)(2,1)}, f32[8,128]{1,0:T(8,128)S(1)}) custom-call(bf16[4,800,4096]{2,1,0:T(8,128)(2,1)S(1)} %get-tuple-element.12.held, f32[4,2,4,7,128]{4,3,2,1,0:T(8,128)S(1)} %get-tuple-element.13.totals, f32[2,8,128]{2,1,0:T(8,128)S(1)} %get-tuple-element.14.totals0, ...), custom_call_target="tpu_custom_call" | custom-call | tf_op jit(solution)/shard_map/finish/pallas_call | solution.py:475
  560.1 14.5 %swap.1.got = bf16[2,288,512]{2,1,0:T(8,128)(2,1)S(1)} custom-call(f32[8,128]{1,0:T(8,128)S(1)} %get-tuple-element.17.after_ref, bf16[2,288,512]{2,1,0:T(8,128)(2,1)S(1)} %get-tuple-element.18.kept), custom_call_target="tpu_custom_call" | custom-call | tf_op jit(solution)/shard_map/swap/pallas_call | solution.py:494
  574.6 0.9 place.1

commit v4 on v3

--- a/solution.py
+++ b/solution.py
@@ -29,7 +29,7 @@
            w_buf, a_buf, staged, sums, parts, halves, sums0, parts0,
            load_sem, load0_sem, send_sem, recv_sem, sum0_send, sum0_recv,
            part_send, part_recv, half_send, half_recv, tot_send, tot_recv,
-           row_send, row_recv, col_send, col_recv, turn_sem):
+           row_send, row_recv, col_send, col_recv, turn_sem, both_sem):
     me, mine = lax.axis_index("rows"), lax.axis_index("owner")
     experts, rows, cols = w_ref.shape
     block = rows // n
@@ -323,6 +323,8 @@
     @pl.when(inner)
     def _():
         block_copy(last - 1, peer(n - turn - 2), me).wait_send()
+        pl.semaphore_signal(both_sem, inc=1, device_id={"owner": mine + 1 - 2 * (mine % 2)}, device_id_type=MESH)
+        pl.semaphore_wait(both_sem, 1)
         pl.semaphore_signal(turn_sem, inc=1, device_id={"rows": peer(quarter)}, device_id_type=MESH)
 
     @pl.when(outer)
@@ -433,7 +435,7 @@
     piece = -(-block // LANES)
     first = LANES * min(2, (block - 1) // LANES)
     middle = block // 2 // LANES * LANES
-    cuts = (middle - LANES, middle, middle + LANES)
+    cuts = (middle - LANES, middle + LANES - 64, middle + LANES)
     tail = pltpu.VMEM((quarter, block - cuts[2], cols), jnp.bfloat16)
     dma = pltpu.SemaphoreType.DMA
     anywhere, vmem = pl.BlockSpec(memory_space=pl.ANY), pl.BlockSpec(memory_space=pltpu.VMEM)
@@ -465,7 +467,7 @@
             dma((experts, quarter)), dma((experts, half)), dma((experts,)), dma((experts,)),
             dma((experts, half)), dma((experts, quarter)),
             dma((n,)), dma((n,)), dma((owners,)), dma((owners,)),
-            pltpu.SemaphoreType.REGULAR,
+            pltpu.SemaphoreType.REGULAR, pltpu.SemaphoreType.REGULAR,
         ],
         compiler_params=pltpu.CompilerParams(
             collective_id=0, has_side_effects=True, vmem_limit_bytes=VMEM_LIMIT
@@ -531,7 +533,7 @@
 
     def per_device(w_down, avg_down, router_weight, router_gain):
         experts, rows, cols = w_down.shape
-        fits = n >= 8 and (n & (n - 1)) == 0 and rows // n >= 4 * LANES and rows % LANES == 0 and rows % (16 * n) == 0 and cols % LANES == 0
+        fits = n >= 8 and owners % 2 == 0 and (n & (n - 1)) == 0 and rows // n >= 4 * LANES and rows % LANES == 0 and rows % (16 * n) == 0 and cols % LANES == 0
         path = with_kernel if fits else with_collectives
         return path(n, owners, w_down, avg_down, router_weight, router_gain)
 

time: 576 us -> 576 us (level)
    pallas_call x1, Pallas kernels: 14.5 us -> 26.1 us  [with_kernel(): pl.pallas_call(functools.partial(swap, n), out_shape=tail, in_specs=[vmem...]
    pallas_call x1, Pallas kernels: 550 us -> 539 us  [with_kernel(): pl.pallas_call(functools.partial(kernel, n, owners, first, cuts), out_sha...]
where the time goes in v4:
time: 576 us
  Pallas kernels  575 us (100%)
    pallas_call x1, Pallas kernels, with_kernel(): pl.pallas_call(functools.partial(kernel, n, owners, first, cuts), out_sha...  539 us
    pallas_call x1, Pallas kernels, with_kernel(): pl.pallas_call(functools.partial(swap, n), out_shape=tail, in_specs=[vmem...  26.1 us

profile of v4, /device:TPU:8, one launch (start us, length us, event | category | flops | bytes accessed | tf_op | source)
XLA Modules:
  0.0 575.7 jit_solution(3972319636561341779)
XLA Ops:
  0.6 539.1 %serve.1 = (bf16[4,800,4096]{2,1,0:T(8,128)(2,1)S(1)}, f32[4,2,4,7,128]{4,3,2,1,0:T(8,128)S(1)}, f32[2,8,128]{2,1,0:T(8,128)S(1)}, bf16[4,8,4,512]{3,2,1,0:T(4,128)(2,1)S(1)}, bf16[2,288,512]{2,1,0:T(8,128)(2,1)S(1)}) custom-call(f32[4,6400,512]{2,1,0:T(8,128)} %w_ref.1, bf16[4,6400,512]{2,1,0:T(8,128)(2,1)} %a_ref.1, f32[4,512]{1,0:T(4,128)} %bitcast.3, ...), custom_call_target="tpu_custom_call" | custom-call | tf_op jit(solution)/shard_map/serve/pallas_call | solution.py:444
  539.8 8.9 %finish.1 = (bf16[4,800,4096]{2,1,0:T(8,128)(2,1)}, f32[4,800]{1,0:T(4,128)}, bf16[16,4096]{1,0:T(8,128)(2,1)}, f32[8,128]{1,0:T(8,128)S(1)}) custom-call(bf16[4,800,4096]{2,1,0:T(8,128)(2,1)S(1)} %get-tuple-element.12.held, f32[4,2,4,7,128]{4,3,2,1,0:T(8,128)S(1)} %get-tuple-element.13.totals, f32[2,8,128]{2,1,0:T(8,128)S(1)} %get-tuple-element.14.totals0, ...), custom_call_target="tpu_custom_call" | custom-call | tf_op jit(solution)/shard_map/finish/pallas_call | solution.py:477
  548.7 26.1 %swap.1.got = bf16[2,288,512]{2,1,0:T(8,128)(2,1)S(1)} custom-call(f32[8,128]{1,0:T(8,128)S(1)} %get-tuple-element.17.after_ref, bf16[2,288,512]{2,1,0:T(8,128)(2,1)S(1)} %get-tuple-element.18.kept), custom_call_target="tpu_custom_call" | custom-call | tf_op jit(solution)/shard_map/swap/pallas_call | solution.py:496
  574.8 0.9 place.1
